TPU v7x, 32 devices: a whole 2x2x4 slice. The times are simulated.
32 devices in a mesh: row: 4 (over y, x), col: 8 (over z, core).
Axes of the slice: x: 2, y: 2, z: 4, core: 2. Of those that a mesh axis runs over, the one named last changes fastest.
Arguments:
- matrix: float32 [2, 4, 256, 1, 8, 256], P(None, 'row', None, None, 'col'), as said below
Outputs:
- factored: float32 [2, 4, 256, 1, 8, 256], P(None, 'row', None, None, 'col')
Inputs may be any that keep to these rules, and one draw needn't show every extreme that they name: `matrix`: symmetric and positive definite.
All inputs are finite; a program needn't handle non-finite values.
Results may differ from a plain program's by a relative error of at most 0.0001.
Values sent between devices are 32-bit elements; how exact they have to be, the bound alone decides.
A program may use at most 128 MiB of HBM per device.

v0:
```python
import jax
import jax.numpy as jnp
from jax import lax
from jax.sharding import PartitionSpec as P

STEPS = 8


def broadcast(value, axis, source):
    kept = jnp.where(lax.axis_index(axis) == source, value, 0).astype(value.dtype)
    return lax.psum(kept, axis)


def solve_panel(factor, column):
    width = column.shape[1]
    inverse = jax.scipy.linalg.solve_triangular(
        factor, jnp.eye(width, dtype=jnp.float32), lower=True
    )
    solved = jnp.einsum("ts,ars->art", inverse, column, precision=lax.Precision.HIGHEST)
    return solved


def on_device(matrix):
    row_tiles = matrix.shape[0]
    width = matrix.shape[2]
    col_tiles = matrix.shape[3]
    tile_grid = matrix.reshape(row_tiles, width, col_tiles, width)
    num_row = lax.axis_size("row")
    num_col = lax.axis_size("col")
    my_row = lax.axis_index("row")
    my_col = lax.axis_index("col")
    rows_global = jnp.arange(row_tiles, dtype=jnp.int32) * num_row + my_row
    ratio = num_col // num_row
    for k in range(STEPS):
        lead_row = k % num_row
        lead_col = k % num_col
        local_row = k // num_row
        local_col = k // num_col
        column = tile_grid[:, :, local_col, :]
        candidate = tile_grid[local_row, :, local_col, :]
        keep = (rows_global > k)[:, None, None]
        diag_tile = broadcast(candidate, "row", lead_row)
        factor = jnp.linalg.cholesky(diag_tile)
        local_panel = jnp.where(keep, solve_panel(factor, column), 0.0)
        panel_rows = broadcast(local_panel, "col", lead_col)
        grouped = panel_rows.reshape(col_tiles, ratio, width, width)
        chosen = lax.dynamic_index_in_dim(grouped, my_col // num_row, 1, keepdims=False)
        panel_cols = broadcast(chosen, "row", my_col % num_row)
        update = jnp.einsum(
            "art,bst->arbs", panel_rows, panel_cols, precision=lax.Precision.HIGHEST
        )
        tile_grid = tile_grid - update
        diagonal_part = jnp.where((rows_global == k)[:, None, None], factor[None], 0.0)
        new_column = panel_rows + diagonal_part
        old_column = tile_grid[:, :, local_col, :]
        tile_grid = tile_grid.at[:, :, local_col, :].set(
            jnp.where(my_col == lead_col, new_column, old_column)
        )
    return tile_grid.reshape(matrix.shape)


def solution(mesh):
    placed = (P(None, "row", None, None, "col", None),)
    return jax.shard_map(
        on_device,
        mesh=mesh,
        in_specs=placed,
        out_specs=P(None, "row", None, None, "col", None),
        check_vma=False,
    )
```

profile of v0, /device:TPU:31, one launch (start us, length us, event | category | flops | bytes accessed | tf_op | source)
XLA Modules:
  0.0 1720.9 jit_solution(9675084317404435007)
XLA Ops:
  9.2 43.7 %all-reduce.26.cloned.1.call-done = f32[256,256]{0,1:T(8,128)} async-done(((f32[256,256]{0,1:T(8,128)}), f32[256,256]{0,1:T(8,128)}) %all-reduce.26.cloned.1.call-update) | async-done | bytes 262160 | tf_op jit(solution)/shard_map/psum | solution.py:11
  116.6 55.2 %all-reduce.28.cloned.1.call-done = f32[2,256,256]{1,2,0:T(8,128)} async-done(((f32[2,256,256]{1,2,0:T(8,128)}), f32[2,256,256]{1,2,0:T(8,128)}) %all-reduce.28.cloned.1.call-update) | async-done | bytes 524304 | tf_op jit(solution)/shard_map/psum | solution.py:11
  174.1 44.1 %all-reduce.30.cloned.1.call-done = f32[256,256]{0,1:T(8,128)} async-done(((f32[256,256]{0,1:T(8,128)}), f32[256,256]{0,1:T(8,128)}) %all-reduce.30.cloned.1.call-update) | async-done | bytes 262160 | tf_op jit(solution)/shard_map/psum | solution.py:11
  220.7 43.4 %all-reduce.32.cloned.1.call-done = f32[256,256]{0,1:T(8,128)} async-done(((f32[256,256]{0,1:T(8,128)}), f32[256,256]{0,1:T(8,128)}) %all-reduce.32.cloned.1.call-update) | async-done | bytes 262160 | tf_op jit(solution)/shard_map/psum | solution.py:11
  338.6 55.3 %all-reduce.34.cloned.1.call-done = f32[2,256,256]{1,2,0:T(8,128)} async-done(((f32[2,256,256]{1,2,0:T(8,128)}), f32[2,256,256]{1,2,0:T(8,128)}) %all-reduce.34.cloned.1.call-update) | async-done | bytes 524304 | tf_op jit(solution)/shard_map/psum | solution.py:11
  395.8 44.3 %all-reduce.36.cloned.1.call-done = f32[256,256]{0,1:T(8,128)} async-done(((f32[256,256]{0,1:T(8,128)}), f32[256,256]{0,1:T(8,128)}) %all-reduce.36.cloned.1.call-update) | async-done | bytes 262160 | tf_op jit(solution)/shard_map/psum | solution.py:11
  442.6 43.5 %all-reduce.38.cloned.1.call-done = f32[256,256]{0,1:T(8,128)} async-done(((f32[256,256]{0,1:T(8,128)}), f32[256,256]{0,1:T(8,128)}) %all-reduce.38.cloned.1.call-update) | async-done | bytes 262160 | tf_op jit(solution)/shard_map/psum | solution.py:11
  550.5 55.3 %all-reduce.40.cloned.1.call-done = f32[2,256,256]{1,2,0:T(8,128)} async-done(((f32[2,256,256]{1,2,0:T(8,128)}), f32[2,256,256]{1,2,0:T(8,128)}) %all-reduce.40.cloned.1.call-update) | async-done | bytes 524304 | tf_op jit(solution)/shard_map/psum | solution.py:11
  607.8 44.5 %all-reduce.42.cloned.1.call-done = f32[256,256]{0,1:T(8,128)} async-done(((f32[256,256]{0,1:T(8,128)}), f32[256,256]{0,1:T(8,128)}) %all-reduce.42.cloned.1.call-update) | async-done | bytes 262160 | tf_op jit(solution)/shard_map/psum | solution.py:11
  654.7 43.4 %all-reduce.44.cloned.1.call-done = f32[256,256]{0,1:T(8,128)} async-done(((f32[256,256]{0,1:T(8,128)}), f32[256,256]{0,1:T(8,128)}) %all-reduce.44.cloned.1.call-update) | async-done | bytes 262160 | tf_op jit(solution)/shard_map/psum | solution.py:11
  762.3 55.3 %all-reduce.46.cloned.1.call-done = f32[2,256,256]{1,2,0:T(8,128)} async-done(((f32[2,256,256]{1,2,0:T(8,128)}), f32[2,256,256]{1,2,0:T(8,128)}) %all-reduce.46.cloned.1.call-update) | async-done | bytes 524304 | tf_op jit(solution)/shard_map/psum | solution.py:11
  819.5 44.3 %all-reduce.48.cloned.1.call-done = f32[256,256]{0,1:T(8,128)} async-done(((f32[256,256]{0,1:T(8,128)}), f32[256,256]{0,1:T(8,128)}) %all-reduce.48.cloned.1.call-update) | async-done | bytes 262160 | tf_op jit(solution)/shard_map/psum | solution.py:11
  866.3 43.5 %all-reduce.50.cloned.1.call-done = f32[256,256]{0,1:T(8,128)} async-done(((f32[256,256]{0,1:T(8,128)}), f32[256,256]{0,1:T(8,128)}) %all-reduce.50.cloned.1.call-update) | async-done | bytes 262160 | tf_op jit(solution)/shard_map/psum | solution.py:11
  974.2 55.3 %all-reduce.52.cloned.1.call-done = f32[2,256,256]{1,2,0:T(8,128)} async-done(((f32[2,256,256]{1,2,0:T(8,128)}), f32[2,256,256]{1,2,0:T(8,128)}) %all-reduce.52.cloned.1.call-update) | async-done | bytes 524304 | tf_op jit(solution)/shard_map/psum | solution.py:11
  1031.4 44.3 %all-reduce.54.cloned.1.call-done = f32[256,256]{0,1:T(8,128)} async-done(((f32[256,256]{0,1:T(8,128)}), f32[256,256]{0,1:T(8,128)}) %all-reduce.54.cloned.1.call-update) | async-done | bytes 262160 | tf_op jit(solution)/shard_map/psum | solution.py:11
  1078.2 43.4 %all-reduce.56.cloned.1.call-done = f32[256,256]{0,1:T(8,128)} async-done(((f32[256,256]{0,1:T(8,128)}), f32[256,256]{0,1:T(8,128)}) %all-reduce.56.cloned.1.call-update) | async-done | bytes 262160 | tf_op jit(solution)/shard_map/psum | solution.py:11
  1185.8 55.3 %all-reduce.58.cloned.1.call-done = f32[2,256,256]{1,2,0:T(8,128)} async-done(((f32[2,256,256]{1,2,0:T(8,128)}), f32[2,256,256]{1,2,0:T(8,128)}) %all-reduce.58.cloned.1.call-update) | async-done | bytes 524304 | tf_op jit(solution)/shard_map/psum | solution.py:11
  1242.9 44.3 %all-reduce.60.cloned.1.call-done = f32[256,256]{0,1:T(8,128)} async-done(((f32[256,256]{0,1:T(8,128)}), f32[256,256]{0,1:T(8,128)}) %all-reduce.60.cloned.1.call-update) | async-done | bytes 262160 | tf_op jit(solution)/shard_map/psum | solution.py:11
  1289.8 43.5 %all-reduce.62.cloned.1.call-done = f32[256,256]{0,1:T(8,128)} async-done(((f32[256,256]{0,1:T(8,128)}), f32[256,256]{0,1:T(8,128)}) %all-reduce.62.cloned.1.call-update) | async-done | bytes 262160 | tf_op jit(solution)/shard_map/psum | solution.py:11
  1397.5 55.3 %all-reduce.64.cloned.1.call-done = f32[2,256,256]{1,2,0:T(8,128)} async-done(((f32[2,256,256]{1,2,0:T(8,128)}), f32[2,256,256]{1,2,0:T(8,128)}) %all-reduce.64.cloned.1.call-update) | async-done | bytes 524304 | tf_op jit(solution)/shard_map/psum | solution.py:11
  1454.7 44.5 %all-reduce.66.cloned.1.call-done = f32[256,256]{0,1:T(8,128)} async-done(((f32[256,256]{0,1:T(8,128)}), f32[256,256]{0,1:T(8,128)}) %all-reduce.66.cloned.1.call-update) | async-done | bytes 262160 | tf_op jit(solution)/shard_map/psum | solution.py:11
  1501.6 43.5 %all-reduce.68.cloned.1.call-done = f32[256,256]{0,1:T(8,128)} async-done(((f32[256,256]{0,1:T(8,128)}), f32[256,256]{0,1:T(8,128)}) %all-reduce.68.cloned.1.call-update) | async-done | bytes 262160 | tf_op jit(solution)/shard_map/psum | solution.py:11
  1609.4 55.3 %all-reduce.70.cloned.1.call-done = f32[2,256,256]{1,2,0:T(8,128)} async-done(((f32[2,256,256]{1,2,0:T(8,128)}), f32[2,256,256]{1,2,0:T(8,128)}) %all-reduce.70.cloned.1.call-update) | async-done | bytes 524304 | tf_op jit(solution)/shard_map/psum | solution.py:11
  1666.5 44.4 %all-reduce.72.cloned.1.call-done = f32[256,256]{0,1:T(8,128)} async-done(((f32[256,256]{0,1:T(8,128)}), f32[256,256]{0,1:T(8,128)}) %all-reduce.72.cloned.1.call-update) | async-done | bytes 262160 | tf_op jit(solution)/shard_map/psum | solution.py:11
  (354 shorter events, 582.3 us)
Async XLA Ops:
  6.5 46.3 %all-reduce.26.cloned.1.call-start = ((), (), s32[]{:S(2)}) async-start(), calls=%async_computation | async-start | bytes 524288 | tf_op jit(solution)/shard_map/psum | solution.py:11
  8.4 163.4 %all-reduce.28.cloned.1.call-start = ((), (), s32[]{:S(2)}) async-start(), calls=%async_computation.1 | async-start | bytes 1048576 | tf_op jit(solution)/shard_map/psum | solution.py:11
  116.5 101.7 %all-reduce.30.cloned.1.call-start = ((), (), s32[]{:S(2)}) async-start(), calls=%async_computation.2 | async-start | bytes 524288 | tf_op jit(solution)/shard_map/psum | solution.py:11
  173.5 90.5 %all-reduce.32.cloned.1.call-start = ((), (), s32[]{:S(2)}) async-start(), calls=%async_computation.3 | async-start | bytes 524288 | tf_op jit(solution)/shard_map/psum | solution.py:11
  220.6 173.3 %all-reduce.34.cloned.1.call-start = ((), (), s32[]{:S(2)}) async-start(), calls=%async_computation.4 | async-start | bytes 1048576 | tf_op jit(solution)/shard_map/psum | solution.py:11
  338.6 101.5 %all-reduce.36.cloned.1.call-start = ((), (), s32[]{:S(2)}) async-start(), calls=%async_computation.5 | async-start | bytes 524288 | tf_op jit(solution)/shard_map/psum | solution.py:11
  395.6 90.5 %all-reduce.38.cloned.1.call-start = ((), (), s32[]{:S(2)}) async-start(), calls=%async_computation.6 | async-start | bytes 524288 | tf_op jit(solution)/shard_map/psum | solution.py:11
  442.5 163.3 %all-reduce.40.cloned.1.call-start = ((), (), s32[]{:S(2)}) async-start(), calls=%async_computation.7 | async-start | bytes 1048576 | tf_op jit(solution)/shard_map/psum | solution.py:11
  550.5 101.8 %all-reduce.42.cloned.1.call-start = ((), (), s32[]{:S(2)}) async-start(), calls=%async_computation.8 | async-start | bytes 524288 | tf_op jit(solution)/shard_map/psum | solution.py:11
  607.6 90.5 %all-reduce.44.cloned.1.call-start = ((), (), s32[]{:S(2)}) async-start(), calls=%async_computation.9 | async-start | bytes 524288 | tf_op jit(solution)/shard_map/psum | solution.py:11
  654.7 162.9 %all-reduce.46.cloned.1.call-start = ((), (), s32[]{:S(2)}) async-start(), calls=%async_computation.10 | async-start | bytes 1048576 | tf_op jit(solution)/shard_map/psum | solution.py:11
  762.2 101.6 %all-reduce.48.cloned.1.call-start = ((), (), s32[]{:S(2)}) async-start(), calls=%async_computation.11 | async-start | bytes 524288 | tf_op jit(solution)/shard_map/psum | solution.py:11
  819.3 90.5 %all-reduce.50.cloned.1.call-start = ((), (), s32[]{:S(2)}) async-start(), calls=%async_computation.12 | async-start | bytes 524288 | tf_op jit(solution)/shard_map/psum | solution.py:11
  866.2 163.3 %all-reduce.52.cloned.1.call-start = ((), (), s32[]{:S(2)}) async-start(), calls=%async_computation.13 | async-start | bytes 1048576 | tf_op jit(solution)/shard_map/psum | solution.py:11
  974.1 101.6 %all-reduce.54.cloned.1.call-start = ((), (), s32[]{:S(2)}) async-start(), calls=%async_computation.14 | async-start | bytes 524288 | tf_op jit(solution)/shard_map/psum | solution.py:11
  1031.2 90.4 %all-reduce.56.cloned.1.call-start = ((), (), s32[]{:S(2)}) async-start(), calls=%async_computation.15 | async-start | bytes 524288 | tf_op jit(solution)/shard_map/psum | solution.py:11
  1078.2 162.9 %all-reduce.58.cloned.1.call-start = ((), (), s32[]{:S(2)}) async-start(), calls=%async_computation.16 | async-start | bytes 1048576 | tf_op jit(solution)/shard_map/psum | solution.py:11
  1185.7 101.6 %all-reduce.60.cloned.1.call-start = ((), (), s32[]{:S(2)}) async-start(), calls=%async_computation.17 | async-start | bytes 524288 | tf_op jit(solution)/shard_map/psum | solution.py:11
  1242.7 90.5 %all-reduce.62.cloned.1.call-start = ((), (), s32[]{:S(2)}) async-start(), calls=%async_computation.18 | async-start | bytes 524288 | tf_op jit(solution)/shard_map/psum | solution.py:11
  1289.7 163.1 %all-reduce.64.cloned.1.call-start = ((), (), s32[]{:S(2)}) async-start(), calls=%async_computation.19 | async-start | bytes 1048576 | tf_op jit(solution)/shard_map/psum | solution.py:11
  1397.4 101.7 %all-reduce.66.cloned.1.call-start = ((), (), s32[]{:S(2)}) async-start(), calls=%async_computation.20 | async-start | bytes 524288 | tf_op jit(solution)/shard_map/psum | solution.py:11
  1454.5 90.7 %all-reduce.68.cloned.1.call-start = ((), (), s32[]{:S(2)}) async-start(), calls=%async_computation.21 | async-start | bytes 524288 | tf_op jit(solution)/shard_map/psum | solution.py:11
  1501.6 163.1 %all-reduce.70.cloned.1.call-start = ((), (), s32[]{:S(2)}) async-start(), calls=%async_computation.22 | async-start | bytes 1048576 | tf_op jit(solution)/shard_map/psum | solution.py:11
  1609.4 101.5 %all-reduce.72.cloned.1.call-start = ((), (), s32[]{:S(2)}) async-start(), calls=%async_computation.23 | async-start | bytes 524288 | tf_op jit(solution)/shard_map/psum | solution.py:11
  (18 other events, 367.9 us)
Sparse Core Ops, SparseCore 0:
  10.3 42.5 all-reduce.25
  116.6 55.1 all-reduce.27
  174.7 43.4 all-reduce.29
  221.0 43.0 all-reduce.31
  338.7 55.1 all-reduce.33
  396.7 43.4 all-reduce.35
  443.1 43.0 all-reduce.37
  550.6 55.2 all-reduce.39
  608.8 43.4 all-reduce.41
  655.0 43.0 all-reduce.43
  762.4 55.1 all-reduce.45
  820.3 43.4 all-reduce.47
  866.7 43.0 all-reduce.49
  974.3 55.2 all-reduce.51
  1032.3 43.4 all-reduce.53
  1078.5 43.0 all-reduce.55
  1185.9 55.1 all-reduce.57
  1243.8 43.4 all-reduce.59
  1290.2 43.0 all-reduce.61
  1397.6 55.1 all-reduce.63
  1455.7 43.4 all-reduce.65
  1502.1 43.0 all-reduce.67
  1609.5 55.1 all-reduce.69
  1667.5 43.4 all-reduce.71
where the time goes:
time: 1730 us; the launch traced here: 1720 us
  waiting for transfers between devices  1150 us (66%)
  other arithmetic  454 us (26%)
  local copies, waits for them, and re-layouts  46.2 us (3%)
  matrix products  35.5 us (2%)
  between operations  26.2 us (2%)
    psum x24, waiting for transfers between devices, broadcast(): return lax.psum(kept, axis)  1140 us
    another operation x55, other arithmetic, on_device(): factor = jnp.linalg.cholesky(diag_tile)  277 us
    another operation x17, other arithmetic, solve_panel(): jax.scipy.linalg.solve_triangular(factor, jnp.eye(width, dtype=jnp.float3...  158 us
  transfers between devices with their start and end apart: 24, of which 24 were waited for; matrix products, arithmetic and copies ran while one was open for 0% of the time, Pallas kernels for 0%

commit v1 on v0

--- a/solution.py
+++ b/solution.py
@@ -1,9 +1,254 @@
+import functools
+
 import jax
 import jax.numpy as jnp
 from jax import lax
+from jax.experimental import pallas as pl
+from jax.experimental.pallas import tpu as pltpu
 from jax.sharding import PartitionSpec as P
 
 STEPS = 8
+LANES = 128
+SUBS = 8
+PANEL = 32
+MESH = pl.DeviceIdType.MESH
+NT = (((1,), (1,)), ((), ()))
+TN = (((0,), (0,)), ((), ()))
+
+
+def split(value):
+    high = value.astype(jnp.bfloat16)
+    low = (value - high.astype(jnp.float32)).astype(jnp.bfloat16)
+    return high, low
+
+
+def dot3(a_high, a_low, b_high, b_low):
+    def one(a, b):
+        return lax.dot_general(a, b, NT, preferred_element_type=jnp.float32)
+
+    return one(a_high, b_high) + (one(a_high, b_low) + one(a_low, b_high))
+
+
+def factor_panel(work, width, base, start):
+    groups = PANEL // SUBS
+    chunks = (width + LANES) // LANES
+    offset = start - base
+    shape = (SUBS, LANES)
+    sub = lax.broadcasted_iota(jnp.int32, shape, 0)
+    rows = []
+    for g in range(groups):
+        at = pl.ds(pl.multiple_of(start + g * SUBS, SUBS), SUBS)
+        row = [work[at, base + h * LANES : base + (h + 1) * LANES] for h in range(chunks)]
+        row.append(pltpu.roll(row[0], lax.rem(LANES - offset, LANES), 1))
+        rows.append(row)
+    for b in range(groups):
+        lane = b * SUBS
+        cols = [
+            [jnp.broadcast_to(rows[g][chunks][:, lane + t : lane + t + 1], shape) for g in range(b, groups)]
+            for t in range(SUBS)
+        ]
+        scales = jnp.ones(shape, jnp.float32)
+        for t in range(SUBS):
+            scale = lax.rsqrt(jnp.broadcast_to(cols[t][0][t : t + 1, :], shape))
+            scales = jnp.where(sub == t, scale, scales)
+            mult = [c * scale for c in cols[t]]
+            for r in range(t + 1, SUBS):
+                across = jnp.broadcast_to(mult[0][r : r + 1, :], shape)
+                cols[r] = [c - m * across for c, m in zip(cols[r], mult)]
+            below = jnp.where(sub > t, mult[0], 0.0)
+            for h in range(chunks + 1):
+                pivot = jnp.broadcast_to(rows[b][h][t : t + 1, :], shape) * scale
+                rows[b][h] = rows[b][h] - below * pivot
+                for g in range(b + 1, groups):
+                    rows[g][h] = rows[g][h] - mult[g - b] * pivot
+        rows[b] = [r * scales for r in rows[b]]
+    for g in range(groups):
+        at = pl.ds(pl.multiple_of(start + g * SUBS, SUBS), SUBS)
+        for h in range(chunks):
+            work[at, base + h * LANES : base + (h + 1) * LANES] = rows[g][h]
+    whole = jnp.concatenate([jnp.concatenate(row[:chunks], 1) for row in rows], 0)
+    high, low = split(whole)
+    rest = width - base
+    left = whole[:, :rest]
+    left = jnp.where(lax.broadcasted_iota(jnp.int32, left.shape, 1) >= offset + PANEL, left, 0.0)
+    left_high, left_low = split(left)
+    update = lax.dot_general(
+        jnp.concatenate([left_high, left_high, left_low], 0),
+        jnp.concatenate([high, low, high], 0),
+        TN,
+        preferred_element_type=jnp.float32,
+    )
+    work[base:width, base : base + width + LANES] -= update
+
+
+def factor_tile(work, width):
+    for base in range(0, width, LANES):
+        def one(i, carry, base=base):
+            factor_panel(work, width, base, base + i * PANEL)
+            return carry
+
+        lax.fori_loop(0, LANES // PANEL, one, 0)
+
+
+def kernel(dims, x_ref, o_ref, tiles, high, low, work, inv_high, inv_low, in_sem, out_sem, send_sem, land_sem):
+    steps, num_row, num_col = dims
+    row_tiles, width, _ = x_ref.shape
+    my_row, my_col = lax.axis_index("row"), lax.axis_index("col")
+    root = jnp.logical_and(my_row == 0, my_col == 0)
+    count = num_row * num_col
+    barrier = pltpu.get_barrier_semaphore()
+
+    def inbound(a, i, slot, device):
+        return pltpu.make_async_remote_copy(
+            src_ref=x_ref.at[a], dst_ref=tiles.at[slot], send_sem=send_sem.at[a], recv_sem=in_sem.at[slot],
+            device_id=device, device_id_type=MESH,
+        )
+
+    def outbound(slot, a, device):
+        return pltpu.make_async_remote_copy(
+            src_ref=tiles.at[slot], dst_ref=o_ref.at[a], send_sem=out_sem.at[slot], recv_sem=land_sem.at[a],
+            device_id=device, device_id_type=MESH,
+        )
+
+    @pl.when(jnp.logical_not(root))
+    def _():
+        pl.semaphore_signal(barrier, inc=1, device_id=(0, 0), device_id_type=MESH)
+        pl.semaphore_wait(barrier, 1)
+        for a in range(row_tiles):
+            i = a * num_row + my_row
+
+            @pl.when(i >= my_col)
+            def _():
+                inbound(a, i, i * steps + my_col, (0, 0)).start()
+
+            @pl.when(i < my_col)
+            def _():
+                o_ref[a] = jnp.zeros((width, width), jnp.float32)
+
+        for a in range(row_tiles):
+            i = a * num_row + my_row
+
+            @pl.when(i >= my_col)
+            def _():
+                inbound(a, i, i * steps + my_col, (0, 0)).wait_send()
+                outbound(0, a, (0, 0)).wait_recv()
+
+    @pl.when(root)
+    def _():
+        for a in range(row_tiles):
+            pltpu.make_async_copy(x_ref.at[a], tiles.at[a * num_row * steps], in_sem.at[a * num_row * steps]).start()
+
+        def greet(d, carry):
+            pl.semaphore_signal(
+                barrier, inc=1, device_id=(d // num_col, lax.rem(d, num_col)), device_id_type=MESH
+            )
+            return carry
+
+        lax.fori_loop(1, count, greet, 0)
+        pl.semaphore_wait(barrier, count - 1)
+
+        def arrive(slot):
+            pltpu.make_async_copy(tiles.at[slot], tiles.at[slot], in_sem.at[slot]).wait()
+
+        def owned(i, k):
+            return jnp.logical_and(lax.rem(i, num_row) == 0, k == 0)
+
+        def send(i, k):
+            slot = i * steps + k
+
+            @pl.when(owned(i, k))
+            def _():
+                pltpu.make_async_copy(tiles.at[slot], o_ref.at[i // num_row], out_sem.at[slot]).start()
+
+            @pl.when(jnp.logical_not(owned(i, k)))
+            def _():
+                outbound(slot, i // num_row, (lax.rem(i, num_row), k)).start()
+
+        def block(i):
+            return pl.ds(pl.multiple_of(i * width, width), width)
+
+        def subtract(i, k):
+            slot = i * steps + k
+            arrive(slot)
+
+            def one(m, carry):
+                tiles[slot] -= dot3(
+                    high[block(i), block(m)], low[block(i), block(m)],
+                    high[block(k), block(m)], low[block(k), block(m)],
+                )
+                return carry
+
+            lax.fori_loop(0, k, one, 0)
+
+        def step(k, carry):
+            slot = k * steps + k
+            subtract(k, k)
+            rows = lax.broadcasted_iota(jnp.int32, (width, width), 0)
+            cols = lax.broadcasted_iota(jnp.int32, (width, width), 1)
+            work[:, :width] = tiles[slot]
+            work[:, width:] = jnp.where(rows == cols, 1.0, 0.0)
+            factor_tile(work, width)
+            tiles[slot] = jnp.where(cols >= rows, work[:, :width], 0.0).T
+            inv_high[...], inv_low[...] = split(work[:, width:])
+
+            def panel(i, carry):
+                subtract(i, k)
+                spot = i * steps + k
+                a_high, a_low = split(tiles[spot])
+                solved = dot3(a_high, a_low, inv_high[...], inv_low[...])
+                tiles[spot] = solved
+                high[block(i), block(k)], low[block(i), block(k)] = split(solved)
+                return carry
+
+            lax.fori_loop(k + 1, steps, panel, 0)
+
+            def ship(i, carry):
+                send(i, k)
+                return carry
+
+            lax.fori_loop(k, steps, ship, 0)
+            return carry
+
+        lax.fori_loop(0, steps, step, 0)
+
+        def finish(k, carry):
+            def one(i, carry):
+                slot = i * steps + k
+                pltpu.make_async_copy(tiles.at[slot], tiles.at[slot], out_sem.at[slot]).wait()
+                return carry
+
+            return lax.fori_loop(k, steps, one, carry)
+
+        lax.fori_loop(0, steps, finish, 0)
+
+
+def on_root(matrix):
+    row_tiles = matrix.shape[0]
+    width = matrix.shape[2]
+    num_row, num_col = lax.axis_size("row"), lax.axis_size("col")
+    order = STEPS * width
+    local = matrix.reshape(row_tiles, width, width)
+    slots = STEPS * STEPS
+    out = pl.pallas_call(
+        functools.partial(kernel, (STEPS, num_row, num_col)),
+        out_shape=jax.ShapeDtypeStruct(local.shape, jnp.float32),
+        in_specs=[pl.BlockSpec(memory_space=pltpu.VMEM)],
+        out_specs=pl.BlockSpec(memory_space=pltpu.VMEM),
+        scratch_shapes=[
+            pltpu.VMEM((slots, width, width), jnp.float32),
+            pltpu.VMEM((order, order), jnp.bfloat16),
+            pltpu.VMEM((order, order), jnp.bfloat16),
+            pltpu.VMEM((width, 2 * width), jnp.float32),
+            pltpu.VMEM((width, width), jnp.bfloat16),
+            pltpu.VMEM((width, width), jnp.bfloat16),
+            pltpu.SemaphoreType.DMA((slots,)),
+            pltpu.SemaphoreType.DMA((slots,)),
+            pltpu.SemaphoreType.DMA((row_tiles,)),
+            pltpu.SemaphoreType.DMA((row_tiles,)),
+        ],
+        compiler_params=pltpu.CompilerParams(collective_id=0, has_side_effects=True, vmem_limit_bytes=56 * 2**20),
+    )(local)
+    return out.reshape(matrix.shape)
 
 
 def broadcast(value, axis, source):
@@ -20,7 +265,7 @@
     return solved
 
 
-def on_device(matrix):
+def stepwise(matrix):
     row_tiles = matrix.shape[0]
     width = matrix.shape[2]
     col_tiles = matrix.shape[3]
@@ -59,6 +304,12 @@
     return tile_grid.reshape(matrix.shape)
 
 
+def on_device(matrix):
+    row_tiles, _, _, col_tiles = matrix.shape[:4]
+    whole = row_tiles * lax.axis_size("row") == STEPS and lax.axis_size("col") == STEPS and col_tiles == 1
+    return on_root(matrix) if whole else stepwise(matrix)
+
+
 def solution(mesh):
     placed = (P(None, "row", None, None, "col", None),)
     return jax.shard_map(

time: 1730 us -> 172 us (0.10)
  waiting for transfers between devices: 1150 us -> 0 us
  other arithmetic: 454 us -> 0 us
  Pallas kernels: 0 us -> 166 us
  local copies, waits for them, and re-layouts: 46.2 us -> 4.24 us
  matrix products: 35.5 us -> 0 us
  between operations: 26.2 us -> 0.01 us
    psum x24 -> x0, waiting for transfers between devices: 1140 us -> none  [broadcast(): return lax.psum(kept, axis)]
    another operation x80 -> x0, other arithmetic: 448 us -> none  [the longest x55 277 us: on_device(): factor = jnp.linalg.cholesky(diag_tile)]
    pallas_call x0 -> x1, Pallas kernels: none -> 166 us  [on_root(): pl.pallas_call(functools.partial(kernel, (STEPS, num_row, num_col)), out_...]
    another operation x74 -> x0, local copies, waits for them, and re-layouts: 33.2 us -> none  [the longest x57 32.6 us: solve_panel(): jax.scipy.linalg.solve_triangular(factor, jnp.eye(width, dtype=jnp.float3...]
    dot_general x16 -> x0, matrix products: 24.6 us -> none  [the longest x8 13.2 us: on_device(): jnp.einsum('art,bst->arbs', panel_rows, panel_cols, precision=lax.Precisi...]
  transfers between devices with their start and end apart: 24 -> 0, of which waited for: 24 -> 0; matrix products, arithmetic and copies ran while one was open for 0% -> 0% of each run, Pallas kernels for 0% -> 0%
where the time goes in v1:
time: 172 us; the launch traced here: 170 us
  Pallas kernels  166 us (97%)
  local copies, waits for them, and re-layouts  4.24 us (2%)
    pallas_call x1, Pallas kernels, on_root(): pl.pallas_call(functools.partial(kernel, (STEPS, num_row, num_col)), out_...  166 us

profile of v1, /device:TPU:31, one launch (start us, length us, event | category | flops | bytes accessed | tf_op | source)
XLA Modules:
  0.0 170.5 jit_solution(8179364723108231464)
XLA Ops:
  0.0 1.9 %copy.5 = f32[2,1,256,1,1,256]{5,2,3,4,1,0:T(8,128)} copy(f32[2,1,256,1,1,256]{5,4,3,2,1,0:T(1,128)} %param.1) | data formatting | bytes 1048576
  1.9 166.2 %shard_map.17 = f32[2,256,256]{2,1,0:T(8,128)} custom-call(f32[2,256,256]{2,1,0:T(8,128)} %bitcast.5), custom_call_target="tpu_custom_call" | custom-call | tf_op jit(solution)/shard_map/pallas_call | solution.py:232
  168.1 2.4 %copy.2 = f32[2,1,256,1,1,256]{5,4,3,2,1,0:T(1,128)} copy(f32[2,1,256,1,1,256]{5,2,0,4,3,1:T(8,128)} %bitcast.4) | data formatting | bytes 1048576 | tf_op jit(solution)/shard_map/reshape | solution.py:251

commit v2 on v1

--- a/solution.py
+++ b/solution.py
@@ -10,7 +10,8 @@
 STEPS = 8
 LANES = 128
 SUBS = 8
-PANEL = 32
+PANEL = 64
+ROOT_COL = 2
 MESH = pl.DeviceIdType.MESH
 NT = (((1,), (1,)), ((), ()))
 TN = (((0,), (0,)), ((), ()))
@@ -90,11 +91,13 @@
         lax.fori_loop(0, LANES // PANEL, one, 0)
 
 
-def kernel(dims, x_ref, o_ref, tiles, high, low, work, inv_high, inv_low, in_sem, out_sem, send_sem, land_sem):
+def kernel(dims, x_ref, o_ref, tiles, high, low, work, inv_high, inv_low, in_sem, out_sem, send_sem, land_sem, go_sem):
     steps, num_row, num_col = dims
     row_tiles, width, _ = x_ref.shape
     my_row, my_col = lax.axis_index("row"), lax.axis_index("col")
-    root = jnp.logical_and(my_row == 0, my_col == 0)
+    root_row, root_col = num_row - 1, min(ROOT_COL, num_col - 1)
+    home = (root_row, root_col)
+    root = jnp.logical_and(my_row == root_row, my_col == root_col)
     count = num_row * num_col
     barrier = pltpu.get_barrier_semaphore()
 
@@ -110,16 +113,31 @@
             device_id=device, device_id_type=MESH,
         )
 
+    beside = my_row == root_row
+    ahead = jnp.where(jnp.logical_and(beside, my_col - 1 == root_col), my_col - 2, my_col - 1)
+    after = jnp.where(jnp.logical_and(beside, my_col + 1 == root_col), my_col + 2, my_col + 1)
+    follows, leads = ahead >= 0, after < num_col
+
     @pl.when(jnp.logical_not(root))
     def _():
-        pl.semaphore_signal(barrier, inc=1, device_id=(0, 0), device_id_type=MESH)
-        pl.semaphore_wait(barrier, 1)
+        pl.semaphore_signal(barrier, inc=1, device_id=home, device_id_type=MESH)
+
+        @pl.when(follows)
+        def _():
+            pl.semaphore_signal(barrier, inc=1, device_id=(my_row, ahead), device_id_type=MESH)
+
+        pl.semaphore_wait(barrier, jnp.where(leads, 2, 1))
+
+        @pl.when(follows)
+        def _():
+            pl.semaphore_wait(go_sem, 1)
+
         for a in range(row_tiles):
             i = a * num_row + my_row
 
             @pl.when(i >= my_col)
             def _():
-                inbound(a, i, i * steps + my_col, (0, 0)).start()
+                inbound(a, i, i * steps + my_col, home).start()
 
             @pl.when(i < my_col)
             def _():
@@ -130,28 +148,44 @@
 
             @pl.when(i >= my_col)
             def _():
-                inbound(a, i, i * steps + my_col, (0, 0)).wait_send()
-                outbound(0, a, (0, 0)).wait_recv()
+                inbound(a, i, i * steps + my_col, home).wait_send()
+
+        @pl.when(leads)
+        def _():
+            pl.semaphore_signal(go_sem, inc=1, device_id=(my_row, after), device_id_type=MESH)
+
+        for a in range(row_tiles):
+            i = a * num_row + my_row
+
+            @pl.when(i >= my_col)
+            def _():
+                outbound(0, a, home).wait_recv()
 
     @pl.when(root)
     def _():
         for a in range(row_tiles):
-            pltpu.make_async_copy(x_ref.at[a], tiles.at[a * num_row * steps], in_sem.at[a * num_row * steps]).start()
+            i = a * num_row + root_row
+            if i >= root_col:
+                slot = i * steps + root_col
+                pltpu.make_async_copy(x_ref.at[a], tiles.at[slot], in_sem.at[slot]).start()
+            else:
+                o_ref[a] = jnp.zeros((width, width), jnp.float32)
 
         def greet(d, carry):
+            d = jnp.where(d >= root_row * num_col + root_col, d + 1, d)
             pl.semaphore_signal(
                 barrier, inc=1, device_id=(d // num_col, lax.rem(d, num_col)), device_id_type=MESH
             )
             return carry
 
-        lax.fori_loop(1, count, greet, 0)
+        lax.fori_loop(0, count - 1, greet, 0)
         pl.semaphore_wait(barrier, count - 1)
 
         def arrive(slot):
             pltpu.make_async_copy(tiles.at[slot], tiles.at[slot], in_sem.at[slot]).wait()
 
         def owned(i, k):
-            return jnp.logical_and(lax.rem(i, num_row) == 0, k == 0)
+            return jnp.logical_and(lax.rem(i, num_row) == root_row, k == root_col)
 
         def send(i, k):
             slot = i * steps + k
@@ -192,6 +226,7 @@
             inv_high[...], inv_low[...] = split(work[:, width:])
 
             def panel(i, carry):
+                send(i - 1, k)
                 subtract(i, k)
                 spot = i * steps + k
                 a_high, a_low = split(tiles[spot])
@@ -202,11 +237,7 @@
 
             lax.fori_loop(k + 1, steps, panel, 0)
 
-            def ship(i, carry):
-                send(i, k)
-                return carry
-
-            lax.fori_loop(k, steps, ship, 0)
+            send(steps - 1, k)
             return carry
 
         lax.fori_loop(0, steps, step, 0)
@@ -245,6 +276,7 @@
             pltpu.SemaphoreType.DMA((slots,)),
             pltpu.SemaphoreType.DMA((row_tiles,)),
             pltpu.SemaphoreType.DMA((row_tiles,)),
+            pltpu.SemaphoreType.REGULAR,
         ],
         compiler_params=pltpu.CompilerParams(collective_id=0, has_side_effects=True, vmem_limit_bytes=56 * 2**20),
     )(local)

time: 172 us -> 126 us (0.73)
  Pallas kernels: 166 us -> 122 us
    pallas_call x1, Pallas kernels: 166 us -> 122 us  [on_root(): pl.pallas_call(functools.partial(kernel, (STEPS, num_row, num_col)), out_...]
where the time goes in v2:
time: 126 us
  Pallas kernels  122 us (97%)
  local copies, waits for them, and re-layouts  4.24 us (3%)
    pallas_call x1, Pallas kernels, on_root(): pl.pallas_call(functools.partial(kernel, (STEPS, num_row, num_col)), out_...  122 us

profile of v2, /device:TPU:31, one launch (start us, length us, event | category | flops | bytes accessed | tf_op | source)
XLA Modules:
  0.0 125.8 jit_solution(18196198617919452692)
XLA Ops:
  0.0 1.9 %copy.5 = f32[2,1,256,1,1,256]{5,2,3,4,1,0:T(8,128)} copy(f32[2,1,256,1,1,256]{5,4,3,2,1,0:T(1,128)} %param.1) | data formatting | bytes 1048576
  1.9 121.5 %shard_map.17 = f32[2,256,256]{2,1,0:T(8,128)} custom-call(f32[2,256,256]{2,1,0:T(8,128)} %bitcast.5), custom_call_target="tpu_custom_call" | custom-call | tf_op jit(solution)/shard_map/pallas_call | solution.py:263
  123.4 2.4 %copy.2 = f32[2,1,256,1,1,256]{5,4,3,2,1,0:T(1,128)} copy(f32[2,1,256,1,1,256]{5,2,0,4,3,1:T(8,128)} %bitcast.4) | data formatting | bytes 1048576 | tf_op jit(solution)/shard_map/reshape | solution.py:283
